TPU v7x, 32 devices: a whole 2x2x4 slice. The times are simulated.
32 devices in a mesh: wide: 8 (over y, x, core), head: 4 (over z).
Axes of the slice: x: 2, y: 2, z: 4, core: 2. Of those that a mesh axis runs over, the one named last changes fastest.
Arguments:
- tokens: bfloat16 [16384, 1024], P(('wide', 'head')), may hold values from -6 to 6
- cotangent: bfloat16 [16384, 1024], P(('wide', 'head')), may hold values from -6 to 6
- w_query: bfloat16 [1024, 1024], P('wide', 'head'), may hold values from -0.25 to 0.25
- w_key: bfloat16 [1024, 1024], P('wide', 'head'), may hold values from -0.25 to 0.25
- w_value: bfloat16 [1024, 1024], P('wide', 'head'), may hold values from -0.1875 to 0.1875
- w_out: bfloat16 [1024, 1024], P('head', 'wide'), may hold values from -0.1875 to 0.1875
- w_up: bfloat16 [1024, 4096], P('wide', 'head'), may hold values from -0.1875 to 0.1875
- w_down: bfloat16 [4096, 1024], P('head', 'wide'), may hold values from -0.09375 to 0.09375
- norm_gain: float32 [4, 1024], replicated, may hold values from 0.25 to 1.75
- norm_bias: float32 [4, 1024], replicated, may hold values from -3 to 3
Outputs:
- block_out: bfloat16 [16384, 1024], P(('wide', 'head'))
- input_grad: float32 [16384, 1024], P(('wide', 'head'))
- grad_query: float32 [1024, 1024], P('wide', 'head')
- grad_key: float32 [1024, 1024], P('wide', 'head')
- grad_value: float32 [1024, 1024], P('wide', 'head')
- grad_out: float32 [1024, 1024], P('head', 'wide')
- grad_up: float32 [1024, 4096], P('wide', 'head')
- grad_down: float32 [4096, 1024], P('head', 'wide')
- gain_grad: float32 [4, 1024], replicated
- bias_grad: float32 [4, 1024], replicated
All inputs are finite; a program needn't handle non-finite values.
Results may differ from a plain program's by a relative error of at most 0.015.
Values may be sent and summed in bfloat16 or wider, within the bound.
No kernel may reach another device: no remote copies, remote signals or barrier semaphores. Data moves between devices by JAX's collectives and lax.ppermute only.
A program may use at most 192 MiB of HBM per device.

v0:
```python
import math
import jax
import jax.numpy as jnp
from jax import lax
from jax.sharding import Mesh, PartitionSpec as P

HD = 64
EPS = 1e-05


def normalize(values, gain, bias):
    average = jnp.mean(values, axis=-1, keepdims=True)
    centred = values - average
    inverse = lax.rsqrt(jnp.mean(centred * centred, axis=-1, keepdims=True) + EPS)
    unit_rows = centred * inverse
    return (unit_rows * gain + bias, unit_rows, inverse)


def normalize_back(gradient, unit_rows, inverse, gain):
    scaled = gradient * gain
    inner_sum = (
        scaled
        - jnp.mean(scaled, axis=-1, keepdims=True)
        - unit_rows * jnp.mean(scaled * unit_rows, axis=-1, keepdims=True)
    )
    return (inner_sum * inverse, jnp.sum(gradient * unit_rows, axis=0), jnp.sum(gradient, axis=0))


def masked_scores(rows_q, key_heads, first_row, score_scale):
    scores = (
        jnp.einsum("qgd,kgd->gqk", rows_q, key_heads, preferred_element_type=jnp.float32)
        * score_scale
    )
    place_q = first_row + jnp.arange(rows_q.shape[0], dtype=jnp.int32)
    place_k = jnp.arange(key_heads.shape[0], dtype=jnp.int32)
    allowed = place_k[None, :] <= place_q[:, None]
    return jnp.where(allowed[None], scores, -1e30)


def attend(queries, key_rows, value_rows, block_rows):
    length, width = queries.shape
    groups = width // HD
    score_scale = 1.0 / math.sqrt(HD)
    query_heads = queries.reshape(length, groups, HD)
    key_heads = key_rows.reshape(length, groups, HD)
    value_heads = value_rows.reshape(length, groups, HD)
    out_blocks = []
    totals = []
    for position in range(length // block_rows):
        first_row = position * block_rows
        last_row = first_row + block_rows
        scores = masked_scores(
            query_heads[first_row:last_row], key_heads[:last_row], first_row, score_scale
        )
        row_max = jnp.max(scores, axis=-1, keepdims=True)
        exp_scores = jnp.exp(scores - row_max)
        row_total = jnp.sum(exp_scores, axis=-1, keepdims=True)
        weights = (exp_scores / row_total).astype(jnp.bfloat16)
        out_blocks.append(
            jnp.einsum(
                "gqk,kgd->qgd", weights, value_heads[:last_row], preferred_element_type=jnp.float32
            )
        )
        totals.append(row_max + jnp.log(row_total))
    return (jnp.concatenate(out_blocks, axis=0).reshape(length, width), totals)


def attend_back(queries, key_rows, value_rows, grad_rows, totals, block_rows):
    length, width = queries.shape
    groups = width // HD
    score_scale = 1.0 / math.sqrt(HD)
    query_heads = queries.reshape(length, groups, HD)
    key_heads = key_rows.reshape(length, groups, HD)
    value_heads = value_rows.reshape(length, groups, HD)
    grad_heads = grad_rows.reshape(length, groups, HD)
    grad_keys = jnp.zeros((length, groups, HD), jnp.float32)
    grad_values = jnp.zeros((length, groups, HD), jnp.float32)
    query_parts = []
    for position in range(length // block_rows):
        first_row = position * block_rows
        last_row = first_row + block_rows
        rows_q = query_heads[first_row:last_row]
        scores = masked_scores(rows_q, key_heads[:last_row], first_row, score_scale)
        weights = jnp.exp(scores - totals[position])
        rounded = weights.astype(jnp.bfloat16)
        grad_block = grad_heads[first_row:last_row]
        grad_values = grad_values.at[:last_row].add(
            jnp.einsum("gqk,qgd->kgd", rounded, grad_block, preferred_element_type=jnp.float32)
        )
        grad_weights = jnp.einsum(
            "qgd,kgd->gqk", grad_block, value_heads[:last_row], preferred_element_type=jnp.float32
        )
        inner_sum = jnp.sum(weights * grad_weights, axis=-1, keepdims=True)
        grad_scores = (weights * (grad_weights - inner_sum)).astype(jnp.bfloat16)
        query_parts.append(
            jnp.einsum(
                "gqk,kgd->qgd",
                grad_scores,
                key_heads[:last_row],
                preferred_element_type=jnp.float32,
            )
            * score_scale
        )
        grad_keys = grad_keys.at[:last_row].add(
            jnp.einsum("gqk,qgd->kgd", grad_scores, rows_q, preferred_element_type=jnp.float32)
            * score_scale
        )
    grad_queries = jnp.concatenate(query_parts, axis=0).reshape(length, width).astype(jnp.bfloat16)
    return (
        grad_queries,
        grad_keys.reshape(length, width).astype(jnp.bfloat16),
        grad_values.reshape(length, width).astype(jnp.bfloat16),
    )


def contract_rows(left_op, right_op):
    return lax.dot_general(
        left_op, right_op, (((0,), (0,)), ((), ())), preferred_element_type=jnp.float32
    )


def contract_cols(left_op, right_op):
    return lax.dot_general(
        left_op, right_op, (((1,), (1,)), ((), ())), preferred_element_type=jnp.float32
    )


WIDE = ("outer", "pair")
ALL = ("outer", "pair", "head")


def swap(values):
    return lax.ppermute(values, "pair", [(0, 1), (1, 0)])


def halves(block, axis):
    size = block.shape[axis] // 2
    place = lax.axis_index("pair")
    own = lax.dynamic_slice_in_dim(block, place * size, size, axis)
    other = lax.dynamic_slice_in_dim(block, (1 - place) * size, size, axis)
    return (own, other)


def in_order(own, other, axis):
    place = lax.axis_index("pair")
    return jnp.where(
        place == 0,
        jnp.concatenate([own, other], axis=axis),
        jnp.concatenate([other, own], axis=axis),
    )


def gather_half(block):
    own, other = halves(block, 1)
    pair_rows = in_order(own, swap(other), 0)
    columns = lax.all_gather(pair_rows, "head", axis=0, tiled=False)
    columns = columns.transpose(1, 0, 2).reshape(pair_rows.shape[0], -1)
    return lax.all_gather(columns, "outer", axis=0, tiled=True)


def scatter_half(grad, groups):
    rows = lax.psum_scatter(grad, "outer", scatter_dimension=0, tiled=True)
    blocks = rows.reshape(rows.shape[0], groups, -1).transpose(1, 0, 2)
    block = lax.psum_scatter(blocks, "head", scatter_dimension=0, tiled=False)
    own, other = halves(block, 0)
    return in_order(own, swap(other), 1)


def on_device(
    tokens, cotangent, w_query, w_key, w_value, w_out, w_up, w_down, norm_gain, norm_bias
):
    groups = lax.axis_size("head")
    rows = tokens.shape[0]
    width = w_query.shape[1]
    bf16 = jnp.bfloat16
    w_attn = lax.all_gather(
        jnp.concatenate([w_query, w_key, w_value], axis=1), WIDE, axis=0, tiled=True
    )
    residual = tokens.astype(jnp.float32)
    norm_a, unit_a, inv_a = normalize(residual, norm_gain[0], norm_bias[0])
    seq_a = lax.all_gather(norm_a.astype(bf16), "head", axis=0, tiled=True)
    full_o = lax.all_gather(
        lax.all_gather(w_out, "head", axis=0, tiled=True).T, WIDE, axis=0, tiled=True
    )
    full_up = gather_half(w_up)
    full_down = gather_half(w_down.T)
    block_rows = min(512, seq_a.shape[0])
    qkv = jnp.dot(seq_a, w_attn, preferred_element_type=jnp.float32).astype(bf16)
    queries, key_rows, value_rows = (qkv[:, i * width : (i + 1) * width] for i in range(3))
    attended, totals = attend(queries, key_rows, value_rows, block_rows)
    attended = lax.all_to_all(
        attended.astype(bf16).reshape(groups, rows, width), "head", 0, 0, tiled=False
    )
    attended = attended.transpose(1, 0, 2).reshape(rows, groups * width)
    mixed = contract_cols(attended, full_o)
    norm_z, unit_z, inv_z = normalize(mixed, norm_gain[1], norm_bias[1])
    hidden = residual + norm_z
    norm_c, unit_c, inv_c = normalize(hidden, norm_gain[2], norm_bias[2])
    rows_c = norm_c.astype(bf16)
    pair_c = jnp.concatenate([rows_c, swap(rows_c)], axis=0)
    pre_act = jnp.dot(pair_c, full_up, preferred_element_type=jnp.float32)
    active, gelu_back = jax.vjp(jax.nn.gelu, pre_act)
    active = active.astype(bf16)
    both = contract_cols(active, full_down)
    output = both[:rows] + swap(both[rows:].astype(bf16)).astype(jnp.float32)
    norm_m, unit_m, inv_m = normalize(output, norm_gain[3], norm_bias[3])
    block_out = (hidden + norm_m).astype(bf16)
    grad_y = cotangent.astype(jnp.float32)
    grad_m, gain_m, bias_m = normalize_back(grad_y, unit_m, inv_m, norm_gain[3])
    rows_gm = grad_m.astype(bf16)
    pair_gm = jnp.concatenate([rows_gm, swap(rows_gm)], axis=0)
    grad_act = jnp.dot(pair_gm, full_down, preferred_element_type=jnp.float32)
    grad_pre = gelu_back(grad_act)[0].astype(bf16)
    both_c = contract_cols(grad_pre, full_up)
    grad_c = both_c[:rows] + swap(both_c[rows:].astype(bf16)).astype(jnp.float32)
    grad_down = scatter_half(contract_rows(pair_gm, active).astype(bf16), groups).T
    grad_up = scatter_half(contract_rows(pair_c, grad_pre).astype(bf16), groups)
    grad_more, gain_c, bias_c = normalize_back(grad_c, unit_c, inv_c, norm_gain[2])
    grad_h = grad_y + grad_more
    grad_z, gain_z, bias_z = normalize_back(grad_h, unit_z, inv_z, norm_gain[1])
    rows_gz = grad_z.astype(bf16)
    grad_att = jnp.dot(rows_gz, full_o, preferred_element_type=jnp.float32).astype(bf16)
    grad_att = grad_att.reshape(rows, groups, width).transpose(1, 0, 2)
    grad_att = lax.all_to_all(grad_att, "head", 0, 0, tiled=False)
    grad_att = grad_att.reshape(groups * rows, width)
    grad_o = contract_rows(rows_gz, attended).astype(bf16)
    grad_o = lax.psum_scatter(grad_o, WIDE, scatter_dimension=0, tiled=True)
    grad_o = grad_o.T.reshape(groups, width, -1)
    grad_o = lax.psum_scatter(grad_o, "head", scatter_dimension=0, tiled=False)
    grad_queries, grad_keys, grad_values = attend_back(
        queries, key_rows, value_rows, grad_att, totals, block_rows
    )
    grad_qkv = jnp.concatenate([grad_queries, grad_keys, grad_values], axis=1)
    grad_a = contract_cols(grad_qkv, w_attn).astype(bf16)
    grad_a = lax.psum_scatter(grad_a, "head", scatter_dimension=0, tiled=True).astype(jnp.float32)
    grad_w = contract_rows(seq_a, grad_qkv).astype(bf16)
    grad_w = lax.psum_scatter(grad_w, WIDE, scatter_dimension=0, tiled=True).astype(jnp.float32)
    grad_first, gain_a, bias_a = normalize_back(grad_a, unit_a, inv_a, norm_gain[0])
    input_grad = grad_h + grad_first
    gain_grad, bias_grad = lax.psum(
        (jnp.stack([gain_a, gain_z, gain_c, gain_m]), jnp.stack([bias_a, bias_z, bias_c, bias_m])),
        ALL,
    )
    return (
        block_out,
        input_grad,
        grad_w[:, :width],
        grad_w[:, width : 2 * width],
        grad_w[:, 2 * width :],
        grad_o.astype(jnp.float32),
        grad_up.astype(jnp.float32),
        grad_down.astype(jnp.float32),
        gain_grad,
        bias_grad,
    )


def solution(mesh):
    wide, head = (mesh.shape["wide"], mesh.shape["head"])
    paired = Mesh(mesh.devices.reshape(wide // 2, 2, head), ALL)
    rows = P(ALL, None)
    by_rows = P(WIDE, "head")
    by_cols = P("head", WIDE)
    in_specs = (rows, rows, by_rows, by_rows, by_rows, by_cols, by_rows, by_cols, P(), P())
    out_specs = (rows, rows, by_rows, by_rows, by_rows, by_cols, by_rows, by_cols, P(), P())
    return jax.shard_map(
        on_device, mesh=paired, in_specs=in_specs, out_specs=out_specs, check_vma=False
    )
```

profile of v0, /device:TPU:0, one launch (start us, length us, event | category | flops | bytes accessed | tf_op | source)
XLA Modules:
  0.0 775.5 jit_solution(3823945687830756972)
XLA Ops:
  18.0 18.6 %all_gather.28 = bf16[1024,128]{1,0:T(8,128)(2,1)} all-gather(bf16[256,128]{1,0:T(8,128)(2,1)S(1)} %copy-done.59), channel_id=1, replica_groups=mesh['outer'=4,'pair'=2,'head'=4] {'head'}, dimensions={0}, use_global_device_ids=true | all-gather | bytes 327680 | tf_op jit(solution)/shard_map/all_gather | solution.py:183
  36.7 9.3 %all-gather.14.cloned.1.call-done = bf16[4,256,512]{2,1,0:T(8,128)(2,1)} async-done(((bf16[1,256,512]{2,1,0:T(8,128)(2,1)}), bf16[4,256,512]{2,1,0:T(8,128)(2,1)}) %all-gather.14.cloned.1.call-update) | async-done | bytes 1048592 | tf_op jit(solution)/shard_map/all_gather | solution.py:156
  46.1 2.3 copy.77
  52.6 22.5 %all-gather.18.cloned.1.call-done = bf16[4,256,512]{2,1,0:T(8,128)(2,1)} async-done(((bf16[1,256,512]{2,1,0:T(8,128)(2,1)}), bf16[4,256,512]{2,1,0:T(8,128)(2,1)}) %all-gather.18.cloned.1.call-update) | async-done | bytes 1048592 | tf_op jit(solution)/shard_map/all_gather | solution.py:156
  75.1 2.3 copy.80
  77.4 24.6 %all-gather.10.cloned.1.call-done = bf16[1024,768]{1,0:T(8,128)(2,1)} async-done(((bf16[128,768]{1,0:T(8,128)(2,1)}), bf16[1024,768]{1,0:T(8,128)(2,1)}) %all-gather.10.cloned.1.call-update) | async-done | bytes 1572880 | tf_op jit(solution)/shard_map/all_gather | solution.py:176
  102.0 82.8 %all-gather.8.cloned.1.call-done = bf16[2048,1024]{1,0:T(8,128)(2,1)} async-done(((bf16[512,1024]{1,0:T(8,128)(2,1)}), bf16[2048,1024]{1,0:T(8,128)(2,1)}) %all-gather.8.cloned.1.call-update) | async-done | bytes 4194320 | tf_op jit(solution)/shard_map/all_gather | solution.py:181
  184.8 6.1 convolution_convert_fusion.3
  201.0 2.9 fusion.108
  204.0 2.5 fusion.132
  208.4 2.6 copy-done
  211.1 4.6 fusion.107
  215.7 7.9 %fusion.131 = (f32[4,512]{1,0:T(4,128)S(1)}, f32[4,512,2048]{2,1,0:T(8,128)}) fusion(bf16[512,4,64]{0,2,1:T(8,128)(2,1)S(1)} %bitcast.227, bf16[2048,4,64]{0,2,1:T(8,128)(2,1)S(1)} %bitcast.211, pred[512,2048]{1,0:T(8,128)(4,1)S(1)} %iota_compare_fusion), kind=kOutput, calls=%fused_computation.230 | convolution fusion | flops 549451776 | bytes 19144704 | tf_op jit(solution)/shard_map/qgd,kgd->gqk/dot_general | solution.py:31
  223.6 8.4 %fusion = f32[4,512]{1,0:T(4,128)S(1)} fusion(f32[4,512,2048]{2,1,0:T(8,128)} %get-tuple-element.223, f32[4,512]{1,0:T(4,128)S(1)} %get-tuple-element.222), kind=kLoop, calls=%fused_computation.6 | loop fusion | flops 8386560 | bytes 16793600 | tf_op jit(solution)/shard_map/reduce_sum | solution.py:57
  232.1 7.6 fusion.106
  243.3 3.5 all-to-all-start
  246.9 25.8 %all-to-all-done = bf16[4,512,256]{1,2,0:T(8,128)(2,1)S(1)} async-done(((bf16[4,512,256]{1,2,0:T(8,128)(2,1)}), bf16[4,512,256]{1,2,0:T(8,128)(2,1)S(1)}, u32[]{:S(2)}, u32[]{:S(2)}) %all-to-all-start) | async-done | bytes 1048608 | tf_op jit(solution)/shard_map/all_to_all | solution.py:191
  272.6 3.3 fusion.135
  278.0 2.7 collective-permute-done
  280.7 10.3 %fusion.85 = f32[1024,2048]{1,0:T(8,128)} fusion(bf16[1024,2048]{0,1:T(8,128)(2,1)} %all-gather.16.cloned.1.call-done, bf16[512,1024]{1,0:T(8,128)(2,1)} %collective-permute-done, bf16[512,1024]{1,0:T(8,128)(2,1)S(1)} %add_convert_fusion.1), kind=kOutput, calls=%fused_computation.139 | convolution fusion | flops 4299161600 | bytes 14680064 | tf_op jit(solution)/shard_map/dot_general | solution.py:201
  291.1 31.1 %all-gather.20.cloned.1.call-done = bf16[1024,2048]{0,1:T(8,128)(2,1)} async-done(((bf16[256,2048]{0,1:T(8,128)(2,1)}), bf16[1024,2048]{0,1:T(8,128)(2,1)}) %all-gather.20.cloned.1.call-update) | async-done | bytes 4194320 | tf_op jit(solution)/shard_map/all_gather | solution.py:158
  322.1 9.0 %fusion.120 = f32[1024,1024]{1,0:T(8,128)S(1)} fusion(bf16[1024,2048]{0,1:T(8,128)(2,1)} %all-gather.20.cloned.1.call-done, f32[1024,2048]{1,0:T(8,128)} %fusion.85), kind=kOutput, calls=%fused_computation.219 | convolution fusion | flops 4313841664 | bytes 16777216 | tf_op jit(solution)/shard_map/dot_general | solution.py:123
  331.3 2.6 collective-permute-done.3
  338.2 2.5 collective-permute-done.4
  340.7 11.2 %fusion.10 = bf16[1024,2048]{1,0:T(8,128)(2,1)} fusion(f32[1024,2048]{1,0:T(8,128)S(1)} %copy-done.73, bf16[1024,2048]{0,1:T(8,128)(2,1)S(1)} %copy-done.70, bf16[512,1024]{1,0:T(8,128)(2,1)S(1)} %collective-permute-done.4, bf16[512,1024]{1,0:T(8,128)(2,1)S(1)} %get-tuple-element.197), kind=kOutput, calls=%fused_computation.24 | convolution fusion | flops 4341104640 | bytes 18874368 | tf_op jit(solution)/shard_map/dot_general | solution.py:212
  351.9 6.3 fusion.136
  358.5 2.6 collective-permute-done.5
  362.7 3.1 multiply_reduce_fusion.5
  368.1 2.7 convolution_convert_fusion.4
  370.8 10.3 %convolution_convert_fusion.1 = bf16[1024,2048]{1,0:T(8,128)(2,1)} fusion(bf16[512,1024]{1,0:T(8,128)(2,1)S(1)} %copy-done.72, bf16[512,1024]{1,0:T(8,128)(2,1)S(1)} %get-tuple-element.197, f32[1024,2048]{1,0:T(8,128)} %fusion.85), kind=kOutput, calls=%fused_computation.51 | convolution fusion | flops 4320133120 | bytes 14680064 | tf_op jit(solution)/shard_map/dot_general | solution.py:117
  382.8 2.5 convolution_convert_fusion.6
  386.4 4.6 all-to-all-start.1
  391.4 9.2 %convolution_convert_fusion.2 = bf16[1024,2048]{1,0:T(8,128)(2,1)} fusion(bf16[1024,2048]{1,0:T(8,128)(2,1)} %fusion.10, bf16[512,1024]{1,0:T(8,128)(2,1)} %collective-permute-done, bf16[512,1024]{1,0:T(8,128)(2,1)S(1)} %copy-done.51), kind=kOutput, calls=%fused_computation.52 | convolution fusion | flops 4301258752 | bytes 10485760 | tf_op jit(solution)/shard_map/dot_general | solution.py:117
  400.7 16.4 %all-to-all-done.1 = bf16[4,512,256]{2,1,0:T(8,128)(2,1)S(1)} async-done(((bf16[4,512,256]{2,1,0:T(8,128)(2,1)}), bf16[4,512,256]{2,1,0:T(8,128)(2,1)S(1)}, u32[]{:S(2)}, u32[]{:S(2)}) %all-to-all-start.1) | async-done | bytes 1048608 | tf_op jit(solution)/shard_map/all_to_all | solution.py:224
  417.3 3.3 multiply_reduce_fusion.3
  428.1 3.8 fusion.92
  431.9 8.2 %multiply_reduce_fusion.2 = (f32[4,512]{1,0:T(4,128)S(1)}, f32[4,512,1024]{2,1,0:T(8,128)}) fusion(f32[4,512,1024]{2,1,0:T(8,128)} %copy-done.1, f32[4,512]{1,0:T(4,128)S(1)} %log_add_fusion.2, bf16[512,4,64]{0,2,1:T(8,128)(2,1)S(1)} %bitcast.237, bf16[1024,4,64]{0,2,1:T(8,128)(2,1)S(1)} %bitcast.246), kind=kOutput, calls=%fused_computation.28 | convolution fusion | flops 274724864 | bytes 17580032 | tf_op jit(solution)/shard_map/qgd,kgd->gqk/dot_general | solution.py:90
  440.9 4.8 multiply_convert_fusion.2
  449.3 6.1 multiply_reduce_fusion.1
  455.3 9.8 %multiply_convert_fusion.1 = bf16[4,512,1536]{2,1,0:T(8,128)(2,1)S(1)} fusion(f32[4,512,1536]{2,1,0:T(8,128)} %get-tuple-element.237, f32[4,512,1536]{2,1,0:T(8,128)} %copy-done, f32[4,512]{1,0:T(4,128)S(1)} %get-tuple-element.236, f32[4,512]{1,0:T(4,128)S(1)} %log_add_fusion.1), kind=kLoop, calls=%fused_computation.8 | loop fusion | flops 12582912 | bytes 31473664 | tf_op jit(solution)/shard_map/convert_element_type | solution.py:94
  465.1 3.2 copy-done.5
  468.3 2.7 fusion.111
  471.6 9.1 %multiply_reduce_fusion = (f32[4,512]{1,0:T(4,128)S(1)}, f32[4,512,2048]{2,1,0:T(8,128)}) fusion(f32[4,512,2048]{2,1,0:T(8,128)S(1)} %bitcast.204, f32[4,512]{1,0:T(4,128)S(1)} %log_add_fusion, bf16[512,4,64]{0,2,1:T(8,128)(2,1)} %bitcast.225, bf16[2048,4,64]{0,2,1:T(8,128)(2,1)S(1)} %bitcast.216), kind=kOutput, calls=%fused_computation.1 | convolution fusion | flops 549451776 | bytes 34881536 | tf_op jit(solution)/shard_map/qgd,kgd->gqk/dot_general | solution.py:90
  480.8 10.4 %multiply_convert_fusion = bf16[4,512,2048]{2,1,0:T(8,128)(2,1)} fusion(f32[4,512,2048]{2,1,0:T(8,128)} %get-tuple-element.239, f32[4,512,2048]{2,1,0:T(8,128)S(1)} %bitcast.204, f32[4,512]{1,0:T(4,128)S(1)} %get-tuple-element.238, f32[4,512]{1,0:T(4,128)S(1)} %log_add_fusion), kind=kLoop, calls=%fused_computation | loop fusion | flops 16777216 | bytes 41959424 | tf_op jit(solution)/shard_map/convert_element_type | solution.py:94
  491.2 7.0 fusion.110
  500.4 4.3 fusion.104
  504.7 4.1 fusion.35
  508.8 2.4 copy.109
  511.4 2.2 fusion.105
  516.4 6.3 fusion.89
  522.7 6.1 fusion.56
  528.9 4.5 fusion.47
  533.3 2.3 copy.110
  535.7 8.3 %fusion.53 = bf16[2048,4,64]{0,2,1:T(8,128)(2,1)S(1)} fusion(f32[2048,4,64]{0,2,1:T(8,128)} %fusion.47, bf16[512,4,64]{0,2,1:T(8,128)(2,1)S(1)} %bitcast.226, f32[4,512,2048]{2,1,0:T(8,128)} %get-tuple-element.223, f32[4,512]{1,0:T(4,128)S(1)} %log_add_fusion), kind=kOutput, calls=%fused_computation.86 | convolution fusion | flops 546308096 | bytes 20193280 | tf_op jit(solution)/shard_map/gqk,qgd->kgd/dot_general | solution.py:88
  544.1 4.7 convolution_convert_fusion.5
  549.1 6.5 convolution_convert_fusion
  557.3 15.8 %reduce-scatter.23.cloned.1.call-done = bf16[1,256,512]{2,1,0:T(8,128)(2,1)} async-done(((bf16[4,256,512]{2,1,0:T(8,128)(2,1)}), bf16[1,256,512]{2,1,0:T(8,128)(2,1)}) %reduce-scatter.23.cloned.1.call-update) | async-done | bytes 262160 | tf_op jit(solution)/shard_map/reduce_scatter | solution.py:164
  574.2 27.0 %reduce-scatter.19.cloned.1.call-done = bf16[1,256,512]{2,1,0:T(8,128)(2,1)} async-done(((bf16[4,256,512]{2,1,0:T(8,128)(2,1)}), bf16[1,256,512]{2,1,0:T(8,128)(2,1)}) %reduce-scatter.19.cloned.1.call-update) | async-done | bytes 262160 | tf_op jit(solution)/shard_map/reduce_scatter | solution.py:164
  602.9 38.3 %reduce-scatter.11.cloned.1.call-done = bf16[128,768]{1,0:T(8,128)(2,1)} async-done(((bf16[1024,768]{1,0:T(8,128)(2,1)}), bf16[128,768]{1,0:T(8,128)(2,1)}) %reduce-scatter.11.cloned.1.call-update) | async-done | bytes 196624 | tf_op jit(solution)/shard_map/reduce_scatter | solution.py:237
  644.7 2.0 copy.94
  648.6 71.6 %reduce-scatter.9.cloned.1.call-done = bf16[512,1024]{1,0:T(8,128)(2,1)} async-done(((bf16[2048,1024]{1,0:T(8,128)(2,1)}), bf16[512,1024]{1,0:T(8,128)(2,1)}) %reduce-scatter.9.cloned.1.call-update) | async-done | bytes 1048592 | tf_op jit(solution)/shard_map/reduce_scatter | solution.py:235
  720.2 2.2 fusion.72
  723.9 41.5 %all-reduce.2 = (f32[4,1024]{1,0:T(4,128)}, f32[4,1024]{1,0:T(4,128)}) all-reduce(f32[4,1024]{1,0:T(4,128)S(1)} %pad_maximum_fusion.14, f32[4,1024]{1,0:T(4,128)S(1)} %pad_maximum_fusion.15), channel_id=1, replica_groups=mesh['outer'=4,'pair'=2,'head'=4] {'outer','pair','head'}, use_global_device_ids=true, to_apply=%region_40.41 | all-reduce | flops 8192 | bytes 65536 | tf_op jit(solution)/shard_map/psum | solution.py:240
  765.4 3.3 fusion.65
  (306 shorter events, 73.5 us)
Async XLA Ops:
  7.2 8.6 %copy-start.9 = (bf16[512,1024]{1,0:T(8,128)(2,1)S(1)}, bf16[512,1024]{1,0:T(8,128)(2,1)}, u32[]{:S(2)}) copy-start(bf16[512,1024]{1,0:T(8,128)(2,1)} %param.30) | copy-start | bytes 3145732
  7.2 9.2 %copy-start.66 = (f32[4,1024]{1,0:T(4,128)S(1)}, f32[4,1024]{1,0:T(4,128)}, u32[]{:S(2)}) copy-start(f32[4,1024]{1,0:T(4,128)} %param.38) | copy-start | bytes 49156
  7.2 9.3 %copy-start.67 = (f32[4,1024]{1,0:T(4,128)S(1)}, f32[4,1024]{1,0:T(4,128)}, u32[]{:S(2)}) copy-start(f32[4,1024]{1,0:T(4,128)} %param.39) | copy-start | bytes 49156
  7.2 38.8 %all-gather.14.cloned.1.call-start = ((), (), s32[]{:S(2)}) async-start(), calls=%async_computation.13 | async-start | bytes 1310720 | tf_op jit(solution)/shard_map/all_gather | solution.py:156
  8.3 1.5 collective-permute-start.1
  9.9 8.1 %copy-start.59 = (bf16[256,128]{1,0:T(8,128)(2,1)S(1)}, bf16[256,128]{1,0:T(8,128)(2,1)}, u32[]{:S(2)}) copy-start(bf16[256,128]{1,0:T(8,128)(2,1)} %param.35) | copy-start | bytes 196612
  10.7 64.5 %all-gather.18.cloned.1.call-start = ((), (), s32[]{:S(2)}) async-start(), calls=%async_computation.15 | async-start | bytes 1310720 | tf_op jit(solution)/shard_map/all_gather | solution.py:156
  11.8 1.4 collective-permute-start.2
  14.0 88.0 %all-gather.10.cloned.1.call-start = ((), (), s32[]{:S(2)}) async-start(), calls=%async_computation.11 | async-start | bytes 1769472 | tf_op jit(solution)/shard_map/all_gather | solution.py:176
  15.7 169.1 %all-gather.8.cloned.1.call-start = ((), (), s32[]{:S(2)}) async-start(), calls=%async_computation.10 | async-start | bytes 5242880 | tf_op jit(solution)/shard_map/all_gather | solution.py:181
  16.0 34.6 %copy-start.62 = (f32[512]{0:T(512)}, f32[512]{0:T(512)S(1)}, u32[]{:S(2)}) copy-start(f32[512]{0:T(512)S(1)} %broadcast_multiply_fusion.11) | copy-start | bytes 6148
  16.4 35.5 %copy-start.64 = (f32[512]{0:T(512)}, f32[512]{0:T(512)S(1)}, u32[]{:S(2)}) copy-start(f32[512]{0:T(512)S(1)} %add_rsqrt_fusion.3) | copy-start | bytes 6148
  16.5 35.5 %copy-start.60 = (f32[1,1024]{1,0:T(1,128)}, f32[1,1024]{1,0:T(1,128)S(1)}, u32[]{:S(2)}) copy-start(f32[1,1024]{1,0:T(1,128)S(1)} %get-tuple-element.216) | copy-start | bytes 12292
  17.9 228.9 %all-gather.12.cloned.1.call-start = ((), (), s32[]{:S(2)}) async-start(), calls=%async_computation.12 | async-start | bytes 2359296 | tf_op jit(solution)/shard_map/all_gather | solution.py:182
  36.7 241.3 %all-gather.16.cloned.1.call-start = ((), (), s32[]{:S(2)}) async-start(), calls=%async_computation.14 | async-start | bytes 5242880 | tf_op jit(solution)/shard_map/all_gather | solution.py:158
  48.4 273.8 %all-gather.20.cloned.1.call-start = ((), (), s32[]{:S(2)}) async-start(), calls=%async_computation.16 | async-start | bytes 5242880 | tf_op jit(solution)/shard_map/all_gather | solution.py:158
  191.0 8.6 %copy-start.44 = (bf16[1024,256]{0,1:T(8,128)(2,1)}, bf16[1024,256]{0,1:T(8,128)(2,1)S(1)}, u32[]{:S(2)}) copy-start(bf16[1024,256]{0,1:T(8,128)(2,1)S(1)} %get-tuple-element.192) | copy-start | bytes 1572868
  192.0 12.0 %copy-start.34 = (bf16[512,256]{0,1:T(8,128)(2,1)}, bf16[512,256]{0,1:T(8,128)(2,1)S(1)}, u32[]{:S(2)}) copy-start(bf16[512,256]{0,1:T(8,128)(2,1)S(1)} %get-tuple-element.187) | copy-start | bytes 786436
  192.0 23.7 %copy-start.26 = (bf16[512,256]{0,1:T(8,128)(2,1)}, bf16[512,256]{0,1:T(8,128)(2,1)S(1)}, u32[]{:S(2)}) copy-start(bf16[512,256]{0,1:T(8,128)(2,1)S(1)} %get-tuple-element.186) | copy-start | bytes 786436
  193.0 11.0 %copy-start.17 = (bf16[1536,256]{0,1:T(8,128)(2,1)}, bf16[1536,256]{0,1:T(8,128)(2,1)S(1)}, u32[]{:S(2)}) copy-start(bf16[1536,256]{0,1:T(8,128)(2,1)S(1)} %get-tuple-element.193) | copy-start | bytes 2359300
  194.3 21.4 %copy-start.14 = (bf16[2048,256]{0,1:T(8,128)(2,1)}, bf16[2048,256]{0,1:T(8,128)(2,1)S(1)}, u32[]{:S(2)}) copy-start(bf16[2048,256]{0,1:T(8,128)(2,1)S(1)} %get-tuple-element.195) | copy-start | bytes 3145732
  223.6 8.5 %copy-start.19 = (bf16[2048,256]{0,1:T(8,128)(2,1)S(1)}, bf16[2048,256]{0,1:T(8,128)(2,1)}, u32[]{:S(2)}) copy-start(bf16[2048,256]{0,1:T(8,128)(2,1)} %get-tuple-element.196) | copy-start | bytes 3145732
  232.1 7.6 copy-start.3
  243.3 29.4 %all-to-all-start = ((bf16[4,512,256]{1,2,0:T(8,128)(2,1)}), bf16[4,512,256]{1,2,0:T(8,128)(2,1)S(1)}, u32[]{:S(2)}, u32[]{:S(2)}) async-start(bf16[4,512,256]{1,2,0:T(8,128)(2,1)} %copy.76), calls=%async_computation | async-start | bytes 2097152 | tf_op jit(solution)/shard_map/all_to_all | solution.py:191
  246.8 251.5 %reduce-scatter.13.cloned.1.call-start = ((), (), s32[]{:S(2)}) async-start(), calls=%async_computation.19 | async-start | bytes 2359296 | tf_op jit(solution)/shard_map/reduce_scatter | solution.py:227
  277.8 13.2 %copy-start.50 = (bf16[512,1024]{1,0:T(8,128)(2,1)}, bf16[512,1024]{1,0:T(8,128)(2,1)S(1)}, u32[]{:S(2)}) copy-start(bf16[512,1024]{1,0:T(8,128)(2,1)S(1)} %add_convert_fusion.1) | copy-start | bytes 3145732
  277.9 2.9 collective-permute-start
  331.3 2.7 collective-permute-start.3
  338.1 13.8 %copy-start.69 = (bf16[1024,2048]{0,1:T(8,128)(2,1)S(1)}, bf16[1024,2048]{0,1:T(8,128)(2,1)}, u32[]{:S(2)}) copy-start(bf16[1024,2048]{0,1:T(8,128)(2,1)} %all-gather.16.cloned.1.call-done) | copy-start | bytes 12582916
  338.1 2.7 collective-permute-start.4
  340.7 11.2 %copy-start.71 = (bf16[512,1024]{1,0:T(8,128)(2,1)}, bf16[512,1024]{1,0:T(8,128)(2,1)S(1)}, u32[]{:S(2)}) copy-start(bf16[512,1024]{1,0:T(8,128)(2,1)S(1)} %collective-permute-done.4) | copy-start | bytes 3145732
  358.4 2.7 collective-permute-start.5
  370.8 138.0 %reduce-scatter.21.cloned.1.call-start = ((), (), s32[]{:S(2)}) async-start(), calls=%async_computation.23 | async-start | bytes 5242880 | tf_op jit(solution)/shard_map/reduce_scatter | solution.py:162
  386.4 30.6 %all-to-all-start.1 = ((bf16[4,512,256]{2,1,0:T(8,128)(2,1)}), bf16[4,512,256]{2,1,0:T(8,128)(2,1)S(1)}, u32[]{:S(2)}, u32[]{:S(2)}) async-start(bf16[4,512,256]{2,1,0:T(8,128)(2,1)} %bitcast.202), calls=%async_computation.1 | async-start | bytes 2097152 | tf_op jit(solution)/shard_map/all_to_all | solution.py:224
  391.0 142.4 %reduce-scatter.17.cloned.1.call-start = ((), (), s32[]{:S(2)}) async-start(), calls=%async_computation.21 | async-start | bytes 5242880 | tf_op jit(solution)/shard_map/reduce_scatter | solution.py:162
  400.6 155.0 %reduce-scatter.15.cloned.1.call-start = ((), (), s32[]{:S(2)}) async-start(), calls=%async_computation.20 | async-start | bytes 327680 | tf_op jit(solution)/shard_map/reduce_scatter | solution.py:229
  426.7 13.4 %copy-start.36 = (bf16[1,512,256]{1,2,0:T(8,128)(2,1)}, bf16[1,512,256]{1,2,0:T(8,128)(2,1)S(1)}, u32[]{:S(2)}) copy-start(bf16[1,512,256]{1,2,0:T(8,128)(2,1)S(1)} %copy.86) | copy-start | bytes 786436
  431.9 8.2 %slice-start.10 = ((s8[8388608]{0:T(1024)(128)(4,1)}), s8[4194304]{0:T(1024)(128)(4,1)S(1)}, s32[]{:S(2)}) async-start(s8[8388608]{0:T(1024)(128)(4,1)} %bitcast.209), calls=%async_computation.35 | async-start | bytes 8388608
  431.9 9.0 %slice-start.11 = ((s8[8388608]{0:T(1024)(128)(4,1)}), s8[4194304]{0:T(1024)(128)(4,1)S(1)}, s32[]{:S(2)}) async-start(s8[8388608]{0:T(1024)(128)(4,1)} %bitcast.209), calls=%async_computation.36 | async-start | bytes 8388608
  440.1 7.8 %slice-start.4 = ((s8[12582912]{0:T(1024)(128)(4,1)}), s8[4194304]{0:T(1024)(128)(4,1)S(1)}, s32[]{:S(2)}) async-start(s8[12582912]{0:T(1024)(128)(4,1)} %bitcast.205), calls=%async_computation.29 | async-start | bytes 8388608
  440.9 8.2 %slice-start.6 = ((s8[12582912]{0:T(1024)(128)(4,1)}), s8[4194304]{0:T(1024)(128)(4,1)S(1)}, s32[]{:S(2)}) async-start(s8[12582912]{0:T(1024)(128)(4,1)} %bitcast.205), calls=%async_computation.31 | async-start | bytes 8388608
  455.3 15.8 %slice-start = ((s8[16777216]{0:T(1024)(128)(4,1)}), s8[4194304]{0:T(1024)(128)(4,1)S(1)}, s32[]{:S(2)}) async-start(s8[16777216]{0:T(1024)(128)(4,1)} %bitcast.203), calls=%async_computation.25 | async-start | bytes 8388608
  455.3 13.0 %copy-start.18 = (bf16[1536,256]{0,1:T(8,128)(2,1)S(1)}, bf16[1536,256]{0,1:T(8,128)(2,1)}, u32[]{:S(2)}) copy-start(bf16[1536,256]{0,1:T(8,128)(2,1)} %copy-done.17) | copy-start | bytes 2359300
  455.3 15.7 %slice-start.1 = ((s8[16777216]{0:T(1024)(128)(4,1)}), s8[4194304]{0:T(1024)(128)(4,1)S(1)}, s32[]{:S(2)}) async-start(s8[16777216]{0:T(1024)(128)(4,1)} %bitcast.203), calls=%async_computation.26 | async-start | bytes 8388608
  455.3 15.7 %slice-start.2 = ((s8[16777216]{0:T(1024)(128)(4,1)}), s8[4194304]{0:T(1024)(128)(4,1)S(1)}, s32[]{:S(2)}) async-start(s8[16777216]{0:T(1024)(128)(4,1)} %bitcast.203), calls=%async_computation.27 | async-start | bytes 8388608
  455.3 15.9 %slice-start.3 = ((s8[16777216]{0:T(1024)(128)(4,1)}), s8[4194304]{0:T(1024)(128)(4,1)S(1)}, s32[]{:S(2)}) async-start(s8[16777216]{0:T(1024)(128)(4,1)} %bitcast.203), calls=%async_computation.28 | async-start | bytes 8388608
  480.8 10.5 %copy-start.15 = (bf16[2048,256]{0,1:T(8,128)(2,1)S(1)}, bf16[2048,256]{0,1:T(8,128)(2,1)}, u32[]{:S(2)}) copy-start(bf16[2048,256]{0,1:T(8,128)(2,1)} %copy-done.14) | copy-start | bytes 3145732
  491.2 9.2 %copy-start.22 = (bf16[1024,256]{0,1:T(8,128)(2,1)S(1)}, bf16[1024,256]{0,1:T(8,128)(2,1)}, u32[]{:S(2)}) copy-start(bf16[1024,256]{0,1:T(8,128)(2,1)} %copy-done.21) | copy-start | bytes 1572868
  500.1 73.0 %reduce-scatter.23.cloned.1.call-start = ((), (), s32[]{:S(2)}) async-start(), calls=%async_computation.24 | async-start | bytes 1310720 | tf_op jit(solution)/shard_map/reduce_scatter | solution.py:164
  511.3 90.0 %reduce-scatter.19.cloned.1.call-start = ((), (), s32[]{:S(2)}) async-start(), calls=%async_computation.22 | async-start | bytes 1310720 | tf_op jit(solution)/shard_map/reduce_scatter | solution.py:164
  511.4 17.5 %slice-start.7 = ((s8[12582912]{0:T(1024)(128)(4,1)}), s8[4194304]{0:T(1024)(128)(4,1)S(1)}, s32[]{:S(2)}) async-start(s8[12582912]{0:T(1024)(128)(4,1)} %bitcast.207), calls=%async_computation.32 | async-start | bytes 8388608
  516.4 12.5 %slice-start.8 = ((s8[12582912]{0:T(1024)(128)(4,1)}), s8[4194304]{0:T(1024)(128)(4,1)S(1)}, s32[]{:S(2)}) async-start(s8[12582912]{0:T(1024)(128)(4,1)} %bitcast.207), calls=%async_computation.33 | async-start | bytes 8388608
  535.6 8.4 %copy-start.47 = (bf16[2048,4,64]{0,2,1:T(8,128)(2,1)S(1)}, bf16[2048,4,64]{0,2,1:T(8,128)(2,1)}, u32[]{:S(2)}) copy-start(bf16[2048,4,64]{0,2,1:T(8,128)(2,1)} %fusion.56) | copy-start | bytes 3145732
  535.6 8.4 %copy-start.52 = (bf16[2048,4,64]{0,2,1:T(8,128)(2,1)S(1)}, bf16[2048,4,64]{0,2,1:T(8,128)(2,1)}, u32[]{:S(2)}) copy-start(bf16[2048,4,64]{0,2,1:T(8,128)(2,1)} %pad_maximum_fusion.12) | copy-start | bytes 3145732
  535.6 105.6 %reduce-scatter.11.cloned.1.call-start = ((), (), s32[]{:S(2)}) async-start(), calls=%async_computation.18 | async-start | bytes 1769472 | tf_op jit(solution)/shard_map/reduce_scatter | solution.py:237
  535.7 8.3 %copy-start.68 = (bf16[2048,1024]{1,0:T(8,128)(2,1)S(1)}, bf16[2048,1024]{1,0:T(8,128)(2,1)}, u32[]{:S(2)}) copy-start(bf16[2048,1024]{1,0:T(8,128)(2,1)} %all-gather.8.cloned.1.call-done) | copy-start | bytes 12582916
  548.8 171.4 %reduce-scatter.9.cloned.1.call-start = ((), (), s32[]{:S(2)}) async-start(), calls=%async_computation.17 | async-start | bytes 5242880 | tf_op jit(solution)/shard_map/reduce_scatter | solution.py:235
  555.6 164.6 %copy-start.10 = (bf16[512,1024]{1,0:T(8,128)(2,1)S(1)}, bf16[512,1024]{1,0:T(8,128)(2,1)}, u32[]{:S(2)}) copy-start(bf16[512,1024]{1,0:T(8,128)(2,1)} %param.30) | copy-start | bytes 3145732
  555.6 164.6 %copy-start.61 = (f32[1,1024]{1,0:T(1,128)S(1)}, f32[1,1024]{1,0:T(1,128)}, u32[]{:S(2)}) copy-start(f32[1,1024]{1,0:T(1,128)} %copy-done.60) | copy-start | bytes 12292
  555.6 164.6 %copy-start.63 = (f32[512]{0:T(512)S(1)}, f32[512]{0:T(512)}, u32[]{:S(2)}) copy-start(f32[512]{0:T(512)} %copy-done.62) | copy-start | bytes 6148
  555.6 164.6 %copy-start.65 = (f32[512]{0:T(512)S(1)}, f32[512]{0:T(512)}, u32[]{:S(2)}) copy-start(f32[512]{0:T(512)} %copy-done.64) | copy-start | bytes 6148
  555.6 209.8 %copy-start.12 = (f32[512,1024]{1,0:T(8,128)S(1)}, f32[512,1024]{1,0:T(8,128)}, u32[]{:S(2)}) copy-start(f32[512,1024]{1,0:T(8,128)} %copy-done.11) | copy-start | bytes 6291460
  574.1 68.8 %collective-permute-start.7 = (bf16[128,512]{1,0:T(8,128)(2,1)S(1)}, bf16[128,512]{1,0:T(8,128)(2,1)}, u32[]{:S(2)}, u32[]{:S(2)}) collective-permute-start(bf16[128,512]{1,0:T(8,128)(2,1)S(1)} %get-tuple-element.204), channel_id=1, source_target_pairs={{0,4},{4,0},{1,5},{5,1},{2,6},{6,2},{3,7},{7,3},{8,12},{12,8},{9,1... | collective-permute-start | bytes 393224 | tf_op jit(solution)/shard_map/ppermute | solution.py:133
  602.9 43.9 %collective-permute-start.6 = (bf16[128,512]{1,0:T(8,128)(2,1)}, bf16[128,512]{1,0:T(8,128)(2,1)}, u32[]{:S(2)}, u32[]{:S(2)}) collective-permute-start(bf16[128,512]{1,0:T(8,128)(2,1)} %get-tuple-element.206), channel_id=1, source_target_pairs={{0,4},{4,0},{1,5},{5,1},{2,6},{6,2},{3,7},{7,3},{8,12},{12,8},{9,1... | collective-permute-start | bytes 393224 | tf_op jit(solution)/shard_map/ppermute | solution.py:133
  (47 other events, 183.7 us)
Sparse Core Ops, SparseCore 0:
  10.8 35.2 all-gather.13
  48.2 26.8 all-gather.17
  77.0 24.9 all-gather.9
  104.0 80.7 all-gather.7
  186.5 26.5 all-gather.11
  214.8 52.4 all-gather.15
  269.7 52.4 all-gather.19
  370.9 41.0 reduce-scatter.12
  415.0 52.5 reduce-scatter.20
  470.4 52.5 reduce-scatter.16
  525.3 19.9 reduce-scatter.14
  547.5 25.5 reduce-scatter.22
  575.4 25.7 reduce-scatter.18
  604.4 36.7 reduce-scatter.10
  643.4 76.7 reduce-scatter.8
where the time goes:
time: 779 us; the launch traced here: 776 us
  waiting for transfers between devices  378 us (49%)
  matrix products  190 us (24%)
  other arithmetic  73 us (9%)
  blocking collectives  60.2 us (8%)
  local copies, waits for them, and re-layouts  48.2 us (6%)
  between operations  15.3 us (2%)
  starting transfers between devices  11.2 us (1%)
    all_gather x1, waiting for transfers between devices, on_device(): seq_a = lax.all_gather(norm_a.astype(bf16), 'head', axis=0, tiled=True)  82.8 us
    reduce_scatter x1, waiting for transfers between devices, on_device(): lax.psum_scatter(grad_a, 'head', scatter_dimension=0, tiled=True)  71.6 us
    reduce_scatter x2, waiting for transfers between devices, scatter_half(): block = lax.psum_scatter(blocks, 'head', scatter_dimension=0, tiled=False)  42.9 us
    psum x1, blocking collectives, on_device(): lax.psum((jnp.stack([gain_a, gain_z, gain_c, gain_m]), jnp.stack([bias_a,...  41.5 us
    reduce_scatter x1, waiting for transfers between devices, on_device(): lax.psum_scatter(grad_w, WIDE, scatter_dimension=0, tiled=True)  38.3 us
    all_gather x2, waiting for transfers between devices, gather_half(): columns = lax.all_gather(pair_rows, 'head', axis=0, tiled=False)  31.8 us
    all_gather x2, waiting for transfers between devices, gather_half(): return lax.all_gather(columns, 'outer', axis=0, tiled=True)  31.1 us
    dot_general x4, matrix products, contract_rows(): lax.dot_general(left_op, right_op, (((0,), (0,)), ((), ())), preferred_el...  26.8 us
  transfers between devices with their start and end apart: 25, of which 17 were waited for; matrix products, arithmetic and copies ran while one was open for 32% of the time, Pallas kernels for 0%

commit v1 on v0

--- a/solution.py
+++ b/solution.py
@@ -3,9 +3,26 @@
 import jax.numpy as jnp
 from jax import lax
 from jax.sharding import Mesh, PartitionSpec as P
+from jax.lax import axis_index, ppermute, psum
 
 HD = 64
 EPS = 1e-05
+
+
+def state_flows_by_axis(field_in):
+    count_all = psum(1, axis_name="head")
+    found = [(dd, (dd + 1) % count_all) for dd in range(count_all)]
+    windows = [(dd, (dd - 1) % count_all) for dd in range(count_all)]
+    y1, tmp = ([field_in], [field_in])
+    for _ in range(count_all // 2):
+        answer = ppermute(y1[-1], axis_name="head", perm=found)
+        y1.append(answer)
+    for _ in range((count_all - 1) // 2):
+        out_arr = ppermute(tmp[-1], axis_name="head", perm=windows)
+        tmp.append(out_arr)
+    view_out = jnp.concatenate([*y1[::-1], *tmp[1:]], axis=0)
+    back = jnp.roll(view_out, (axis_index("head") - count_all // 2) * field_in.shape[0], axis=0)
+    return back
 
 
 def normalize(values, gain, bias):
@@ -178,7 +195,7 @@
     )
     residual = tokens.astype(jnp.float32)
     norm_a, unit_a, inv_a = normalize(residual, norm_gain[0], norm_bias[0])
-    seq_a = lax.all_gather(norm_a.astype(bf16), "head", axis=0, tiled=True)
+    seq_a = state_flows_by_axis(norm_a.astype(bf16))
     full_o = lax.all_gather(
         lax.all_gather(w_out, "head", axis=0, tiled=True).T, WIDE, axis=0, tiled=True
     )

time: 779 us -> 725 us (0.931)
  waiting for transfers between devices: 378 us -> 306 us
  starting transfers between devices: 11.2 us -> 21.3 us
  local copies, waits for them, and re-layouts: 48.2 us -> 57.2 us
    all_gather x1 -> x0, waiting for transfers between devices: 82.8 us -> none  [on_device(): seq_a = lax.all_gather(norm_a.astype(bf16), 'head', axis=0, tiled=True)]
    ppermute x0 -> x3, waiting for transfers between devices: none -> 72 us  [the longest x2 72 us: state_flows_by_axis(): answer = ppermute(y1[-1], axis_name='head', perm=found)]
    all_gather x1, waiting for transfers between devices: 24.6 us -> 0.01 us  [on_device(): lax.all_gather(jnp.concatenate([w_query, w_key, w_value], axis=1), WIDE,...]
    all_gather x2, waiting for transfers between devices: 31.1 us -> 6.91 us  [gather_half(): return lax.all_gather(columns, 'outer', axis=0, tiled=True)]
    all_gather x2, waiting for transfers between devices: 31.8 us -> 9.67 us  [gather_half(): columns = lax.all_gather(pair_rows, 'head', axis=0, tiled=False)]
    ppermute x0 -> x3, starting transfers between devices: none -> 10.3 us  [the longest x2 7.22 us: state_flows_by_axis(): answer = ppermute(y1[-1], axis_name='head', perm=found)]
    unnamed x175 -> x168, local copies, waits for them, and re-layouts: 18.6 us -> 27.2 us
    reduce_scatter x2, waiting for transfers between devices: 42.9 us -> 50.7 us  [scatter_half(): block = lax.psum_scatter(blocks, 'head', scatter_dimension=0, tiled=False)]
  transfers between devices with their start and end apart: 25 -> 27, of which waited for: 17 -> 17; matrix products, arithmetic and copies ran while one was open for 32% -> 36% of each run, Pallas kernels for 0% -> 0%
where the time goes in v1:
time: 725 us; the launch traced here: 721 us
  waiting for transfers between devices  306 us (42%)
  matrix products  185 us (26%)
  other arithmetic  75.2 us (10%)
  blocking collectives  60.9 us (8%)
  local copies, waits for them, and re-layouts  57.2 us (8%)
  starting transfers between devices  21.3 us (3%)
  between operations  15.2 us (2%)
    ppermute x2, waiting for transfers between devices, state_flows_by_axis(): answer = ppermute(y1[-1], axis_name='head', perm=found)  72 us
    reduce_scatter x1, waiting for transfers between devices, on_device(): lax.psum_scatter(grad_a, 'head', scatter_dimension=0, tiled=True)  71.6 us
    reduce_scatter x2, waiting for transfers between devices, scatter_half(): block = lax.psum_scatter(blocks, 'head', scatter_dimension=0, tiled=False)  50.7 us
    psum x1, blocking collectives, on_device(): lax.psum((jnp.stack([gain_a, gain_z, gain_c, gain_m]), jnp.stack([bias_a,...  41.5 us
    reduce_scatter x1, waiting for transfers between devices, on_device(): lax.psum_scatter(grad_w, WIDE, scatter_dimension=0, tiled=True)  38.5 us
    dot_general x4, matrix products, contract_rows(): lax.dot_general(left_op, right_op, (((0,), (0,)), ((), ())), preferred_el...  29.1 us
    unnamed x168, local copies, waits for them, and re-layouts  27.2 us
    convert_element_type x4, other arithmetic, attend_back(): grad_scores = (weights * (grad_weights - inner_sum)).astype(jnp.bfloat16)  26.8 us
  transfers between devices with their start and end apart: 27, of which 17 were waited for; matrix products, arithmetic and copies ran while one was open for 36% of the time, Pallas kernels for 0%

profile of v1, /device:TPU:0, one launch (start us, length us, event | category | flops | bytes accessed | tf_op | source)
XLA Modules:
  0.0 720.6 jit_solution(3128145378018568035)
XLA Ops:
  15.8 19.5 %all_gather.24 = bf16[1024,128]{1,0:T(8,128)(2,1)} all-gather(bf16[256,128]{1,0:T(8,128)(2,1)} %param.35), channel_id=1, replica_groups=mesh['outer'=4,'pair'=2,'head'=4] {'head'}, dimensions={0}, use_global_device_ids=true | all-gather | bytes 327680 | tf_op jit(solution)/shard_map/all_gather | solution.py:200
  35.3 9.6 %all-gather.11.cloned.1.call-done = bf16[4,256,512]{2,1,0:T(8,128)(2,1)} async-done(((bf16[1,256,512]{2,1,0:T(8,128)(2,1)}), bf16[4,256,512]{2,1,0:T(8,128)(2,1)}) %all-gather.11.cloned.1.call-update) | async-done | bytes 1048592 | tf_op jit(solution)/shard_map/all_gather | solution.py:173
  50.1 3.1 collective-permute-start.2
  55.2 39.2 %collective-permute-done = bf16[512,1024]{1,0:T(8,128)(2,1)} collective-permute-done((bf16[512,1024]{1,0:T(8,128)(2,1)}, bf16[512,1024]{1,0:T(8,128)(2,1)}, u32[]{:S(2)}, u32[]{:S(2)}) %collective-permute-start) | collective-permute-done | bytes 1048608 | tf_op jit(solution)/shard_map/ppermute | solution.py:18
  94.4 6.5 collective-permute-start.1
  105.4 32.8 %collective-permute-done.1 = bf16[512,1024]{1,0:T(8,128)(2,1)} collective-permute-done((bf16[512,1024]{1,0:T(8,128)(2,1)}, bf16[512,1024]{1,0:T(8,128)(2,1)}, u32[]{:S(2)}, u32[]{:S(2)}) %collective-permute-start.1) | collective-permute-done | bytes 1048608 | tf_op jit(solution)/shard_map/ppermute | solution.py:18
  138.1 2.3 constant_dynamic-update-slice_fusion.7
  140.5 2.3 constant_dynamic-update-slice_fusion.6
  144.2 2.3 constant_dynamic-update-slice_fusion.4
  146.4 2.3 constant_dynamic-update-slice_fusion.3
  148.8 2.3 constant_dynamic-update-slice_fusion.2
  152.5 2.3 constant_dynamic-update-slice_fusion
  154.8 6.1 fusion.30
  171.1 3.0 fusion.118
  174.1 2.5 fusion.144
  178.5 2.6 copy-done
  181.1 4.6 fusion.117
  185.7 7.8 %fusion.143 = (f32[4,512]{1,0:T(4,128)S(1)}, f32[4,512,2048]{2,1,0:T(8,128)}) fusion(bf16[512,4,64]{0,2,1:T(8,128)(2,1)S(1)} %bitcast.223, bf16[2048,4,64]{0,2,1:T(8,128)(2,1)S(1)} %bitcast.207, pred[512,2048]{1,0:T(8,128)(4,1)S(1)} %iota_compare_fusion), kind=kOutput, calls=%fused_computation.244 | convolution fusion | flops 549451776 | bytes 19144704 | tf_op jit(solution)/shard_map/qgd,kgd->gqk/dot_general | solution.py:48
  193.5 8.2 %fusion = f32[4,512]{1,0:T(4,128)S(1)} fusion(f32[4,512,2048]{2,1,0:T(8,128)} %get-tuple-element.223, f32[4,512]{1,0:T(4,128)S(1)} %get-tuple-element.222), kind=kLoop, calls=%fused_computation.6 | loop fusion | flops 8386560 | bytes 16793600 | tf_op jit(solution)/shard_map/reduce_sum | solution.py:74
  201.8 7.6 %fusion.116 = bf16[512,4,64]{0,2,1:T(8,128)(2,1)S(1)} fusion(bf16[2048,4,64]{0,2,1:T(8,128)(2,1)S(1)} %bitcast.211, f32[4,512,2048]{2,1,0:T(8,128)} %get-tuple-element.223, f32[4,512]{1,0:T(4,128)S(1)} %fusion, f32[4,512]{1,0:T(4,128)S(1)} %get-tuple-element.222), kind=kOutput, calls=%fused_computation.163 | convolution fusion | flops 549584896 | bytes 18104320 | tf_op jit(solution)/shard_map/gqk,kgd->qgd/dot_general | solution.py:77
  213.0 3.5 all-to-all-start
  216.6 25.1 %all-to-all-done = bf16[4,512,256]{1,2,0:T(8,128)(2,1)S(1)} async-done(((bf16[4,512,256]{1,2,0:T(8,128)(2,1)}), bf16[4,512,256]{1,2,0:T(8,128)(2,1)S(1)}, u32[]{:S(2)}, u32[]{:S(2)}) %all-to-all-start) | async-done | bytes 1048608 | tf_op jit(solution)/shard_map/all_to_all | solution.py:208
  241.7 3.4 fusion.147
  247.0 2.8 collective-permute-done.3
  249.8 10.3 %fusion.95 = f32[1024,2048]{1,0:T(8,128)} fusion(bf16[1024,2048]{0,1:T(8,128)(2,1)} %all-gather.13.cloned.1.call-done, bf16[512,1024]{1,0:T(8,128)(2,1)} %collective-permute-done.3, bf16[512,1024]{1,0:T(8,128)(2,1)S(1)} %add_convert_fusion.1), kind=kOutput, calls=%fused_computation.143 | convolution fusion | flops 4299161600 | bytes 14680064 | tf_op jit(solution)/shard_map/dot_general | solution.py:218
  260.2 6.9 all-gather.17.cloned.1.call-done
  267.1 9.0 %fusion.132 = f32[1024,1024]{1,0:T(8,128)S(1)} fusion(bf16[1024,2048]{0,1:T(8,128)(2,1)} %all-gather.17.cloned.1.call-done, f32[1024,2048]{1,0:T(8,128)} %fusion.95), kind=kOutput, calls=%fused_computation.233 | convolution fusion | flops 4313841664 | bytes 16777216 | tf_op jit(solution)/shard_map/dot_general | solution.py:140
  276.3 2.6 collective-permute-done.6
  283.1 2.5 collective-permute-done.7
  285.7 11.2 %fusion.10 = bf16[1024,2048]{1,0:T(8,128)(2,1)} fusion(f32[1024,2048]{1,0:T(8,128)S(1)} %copy-done.70, bf16[1024,2048]{0,1:T(8,128)(2,1)S(1)} %copy-done.67, bf16[512,1024]{1,0:T(8,128)(2,1)S(1)} %collective-permute-done.7, bf16[512,1024]{1,0:T(8,128)(2,1)S(1)} %get-tuple-element.197), kind=kOutput, calls=%fused_computation.24 | convolution fusion | flops 4341104640 | bytes 18874368 | tf_op jit(solution)/shard_map/dot_general | solution.py:229
  296.9 6.3 fusion.148
  303.5 2.5 collective-permute-done.8
  307.6 3.1 multiply_reduce_fusion.5
  313.0 2.7 convolution_convert_fusion.3
  315.8 10.2 %convolution_convert_fusion.1 = bf16[1024,2048]{1,0:T(8,128)(2,1)} fusion(bf16[512,1024]{1,0:T(8,128)(2,1)S(1)} %copy-done.69, bf16[512,1024]{1,0:T(8,128)(2,1)S(1)} %get-tuple-element.197, f32[1024,2048]{1,0:T(8,128)} %fusion.95), kind=kOutput, calls=%fused_computation.51 | convolution fusion | flops 4320133120 | bytes 14680064 | tf_op jit(solution)/shard_map/dot_general | solution.py:134
  330.3 4.6 all-to-all-start.1
  335.3 9.4 %convolution_convert_fusion.2 = bf16[1024,2048]{1,0:T(8,128)(2,1)} fusion(bf16[1024,2048]{1,0:T(8,128)(2,1)} %fusion.10, bf16[512,1024]{1,0:T(8,128)(2,1)} %collective-permute-done.3, bf16[512,1024]{1,0:T(8,128)(2,1)S(1)} %copy-done.49), kind=kOutput, calls=%fused_computation.52 | convolution fusion | flops 4301258752 | bytes 10485760 | tf_op jit(solution)/shard_map/dot_general | solution.py:134
  344.8 16.1 %all-to-all-done.1 = bf16[4,512,256]{2,1,0:T(8,128)(2,1)S(1)} async-done(((bf16[4,512,256]{2,1,0:T(8,128)(2,1)}), bf16[4,512,256]{2,1,0:T(8,128)(2,1)S(1)}, u32[]{:S(2)}, u32[]{:S(2)}) %all-to-all-start.1) | async-done | bytes 1048608 | tf_op jit(solution)/shard_map/all_to_all | solution.py:241
  362.3 3.3 multiply_reduce_fusion.3
  370.9 4.5 multiply_reduce_fusion.2
  375.3 4.7 multiply_convert_fusion.2
  384.9 6.1 multiply_reduce_fusion.1
  391.0 10.6 %multiply_convert_fusion.1 = bf16[4,512,1536]{2,1,0:T(8,128)(2,1)S(1)} fusion(f32[4,512,1536]{2,1,0:T(8,128)} %get-tuple-element.237, f32[4,512,1536]{2,1,0:T(8,128)} %copy-done, f32[4,512]{1,0:T(4,128)S(1)} %get-tuple-element.236, f32[4,512]{1,0:T(4,128)S(1)} %log_add_fusion.1), kind=kLoop, calls=%fused_computation.8 | loop fusion | flops 12582912 | bytes 31473664 | tf_op jit(solution)/shard_map/convert_element_type | solution.py:111
  401.7 2.7 fusion.121
  405.8 7.8 %multiply_reduce_fusion = (f32[4,512]{1,0:T(4,128)S(1)}, f32[4,512,2048]{2,1,0:T(8,128)}) fusion(f32[4,512,2048]{2,1,0:T(8,128)S(1)} %bitcast.202, f32[4,512]{1,0:T(4,128)S(1)} %log_add_fusion, bf16[512,4,64]{0,2,1:T(8,128)(2,1)S(1)} %bitcast.221, bf16[2048,4,64]{0,2,1:T(8,128)(2,1)S(1)} %bitcast.212), kind=kOutput, calls=%fused_computation.1 | convolution fusion | flops 549451776 | bytes 34881536 | tf_op jit(solution)/shard_map/qgd,kgd->gqk/dot_general | solution.py:107
  413.6 10.3 %multiply_convert_fusion = bf16[4,512,2048]{2,1,0:T(8,128)(2,1)} fusion(f32[4,512,2048]{2,1,0:T(8,128)} %get-tuple-element.239, f32[4,512,2048]{2,1,0:T(8,128)S(1)} %bitcast.202, f32[4,512]{1,0:T(4,128)S(1)} %get-tuple-element.238, f32[4,512]{1,0:T(4,128)S(1)} %log_add_fusion), kind=kLoop, calls=%fused_computation | loop fusion | flops 16777216 | bytes 41959424 | tf_op jit(solution)/shard_map/convert_element_type | solution.py:111
  426.1 4.3 fusion.114
  432.0 6.4 fusion.99
  438.4 2.4 copy.109
  440.9 2.8 fusion.115
  443.8 6.9 fusion.120
  450.7 6.6 fusion.63
  457.3 8.5 %fusion.54 = f32[2048,4,64]{0,2,1:T(8,128)} fusion(f32[2048,4,64]{0,2,1:T(8,128)} %fusion.99, bf16[512,4,64]{0,2,1:T(8,128)(2,1)S(1)} %bitcast.230, f32[4,512,1536]{2,1,0:T(8,128)} %copy-done, f32[4,512]{1,0:T(4,128)S(1)} %log_add_fusion.1), kind=kOutput, calls=%fused_computation.88 | convolution fusion | flops 409337856 | bytes 15998976 | tf_op jit(solution)/shard_map/gqk,qgd->kgd/dot_general | solution.py:105
  465.7 2.5 reduce-scatter.17.cloned.1.call-done
  468.2 2.3 copy.110
  471.0 8.2 %fusion.60 = bf16[2048,4,64]{0,2,1:T(8,128)(2,1)S(1)} fusion(f32[2048,4,64]{0,2,1:T(8,128)} %fusion.54, bf16[512,4,64]{0,2,1:T(8,128)(2,1)S(1)} %bitcast.222, f32[4,512,2048]{2,1,0:T(8,128)} %get-tuple-element.223, f32[4,512]{1,0:T(4,128)S(1)} %log_add_fusion), kind=kOutput, calls=%fused_computation.90 | convolution fusion | flops 546308096 | bytes 20193280 | tf_op jit(solution)/shard_map/gqk,qgd->kgd/dot_general | solution.py:105
  479.3 6.9 fusion.85
  486.2 6.5 convolution_convert_fusion
  494.4 23.8 %reduce-scatter.23.cloned.1.call-done = bf16[1,256,512]{2,1,0:T(8,128)(2,1)} async-done(((bf16[4,256,512]{2,1,0:T(8,128)(2,1)}), bf16[1,256,512]{2,1,0:T(8,128)(2,1)}) %reduce-scatter.23.cloned.1.call-update) | async-done | bytes 262160 | tf_op jit(solution)/shard_map/reduce_scatter | solution.py:181
  519.3 26.9 %reduce-scatter.19.cloned.1.call-done = bf16[1,256,512]{2,1,0:T(8,128)(2,1)} async-done(((bf16[4,256,512]{2,1,0:T(8,128)(2,1)}), bf16[1,256,512]{2,1,0:T(8,128)(2,1)}) %reduce-scatter.19.cloned.1.call-update) | async-done | bytes 262160 | tf_op jit(solution)/shard_map/reduce_scatter | solution.py:181
  547.8 38.5 %reduce-scatter.11.cloned.1.call-done = bf16[128,768]{1,0:T(8,128)(2,1)} async-done(((bf16[1024,768]{1,0:T(8,128)(2,1)}), bf16[128,768]{1,0:T(8,128)(2,1)}) %reduce-scatter.11.cloned.1.call-update) | async-done | bytes 196624 | tf_op jit(solution)/shard_map/reduce_scatter | solution.py:254
  593.7 71.6 %reduce-scatter.9.cloned.1.call-done = bf16[512,1024]{1,0:T(8,128)(2,1)} async-done(((bf16[2048,1024]{1,0:T(8,128)(2,1)}), bf16[512,1024]{1,0:T(8,128)(2,1)}) %reduce-scatter.9.cloned.1.call-update) | async-done | bytes 1048592 | tf_op jit(solution)/shard_map/reduce_scatter | solution.py:252
  669.1 41.5 %all-reduce.2 = (f32[4,1024]{1,0:T(4,128)}, f32[4,1024]{1,0:T(4,128)}) all-reduce(f32[4,1024]{1,0:T(4,128)S(1)} %pad_maximum_fusion.14, f32[4,1024]{1,0:T(4,128)S(1)} %pad_maximum_fusion.15), channel_id=1, replica_groups=mesh['outer'=4,'pair'=2,'head'=4] {'outer','pair','head'}, use_global_device_ids=true, to_apply=%region_40.41 | all-reduce | flops 8192 | bytes 65536 | tf_op jit(solution)/shard_map/psum | solution.py:257
  710.5 3.3 fusion.72
  (304 shorter events, 86.3 us)
Async XLA Ops:
  7.2 40.1 %copy-start.5 = (bf16[512,1024]{1,0:T(8,128)(2,1)S(1)}, bf16[512,1024]{1,0:T(8,128)(2,1)}, u32[]{:S(2)}) copy-start(bf16[512,1024]{1,0:T(8,128)(2,1)} %param.30) | copy-start | bytes 3145732
  7.2 37.7 %all-gather.11.cloned.1.call-start = ((), (), s32[]{:S(2)}) async-start(), calls=%async_computation.12 | async-start | bytes 1310720 | tf_op jit(solution)/shard_map/all_gather | solution.py:173
  8.3 1.5 collective-permute-start.4
  10.6 37.3 %copy-start.64 = (f32[4,1024]{1,0:T(4,128)S(1)}, f32[4,1024]{1,0:T(4,128)}, u32[]{:S(2)}) copy-start(f32[4,1024]{1,0:T(4,128)} %param.38) | copy-start | bytes 49156
  10.7 37.3 %copy-start.65 = (f32[4,1024]{1,0:T(4,128)S(1)}, f32[4,1024]{1,0:T(4,128)}, u32[]{:S(2)}) copy-start(f32[4,1024]{1,0:T(4,128)} %param.39) | copy-start | bytes 49156
  10.7 92.4 %all-gather.15.cloned.1.call-start = ((), (), s32[]{:S(2)}) async-start(), calls=%async_computation.14 | async-start | bytes 1310720 | tf_op jit(solution)/shard_map/all_gather | solution.py:173
  11.8 1.4 collective-permute-start.5
  14.0 140.8 %all-gather.7.cloned.1.call-start = ((), (), s32[]{:S(2)}) async-start(), calls=%async_computation.10 | async-start | bytes 1769472 | tf_op jit(solution)/shard_map/all_gather | solution.py:193
  15.7 200.8 %all-gather.9.cloned.1.call-start = ((), (), s32[]{:S(2)}) async-start(), calls=%async_computation.11 | async-start | bytes 2359296 | tf_op jit(solution)/shard_map/all_gather | solution.py:199
  35.2 214.6 %all-gather.13.cloned.1.call-start = ((), (), s32[]{:S(2)}) async-start(), calls=%async_computation.13 | async-start | bytes 5242880 | tf_op jit(solution)/shard_map/all_gather | solution.py:175
  47.2 219.9 %all-gather.17.cloned.1.call-start = ((), (), s32[]{:S(2)}) async-start(), calls=%async_computation.15 | async-start | bytes 5242880 | tf_op jit(solution)/shard_map/all_gather | solution.py:175
  47.5 103.6 %copy-start.60 = (f32[512]{0:T(512)}, f32[512]{0:T(512)S(1)}, u32[]{:S(2)}) copy-start(f32[512]{0:T(512)S(1)} %broadcast_multiply_fusion.11) | copy-start | bytes 6148
  47.9 103.2 %copy-start.62 = (f32[512]{0:T(512)}, f32[512]{0:T(512)S(1)}, u32[]{:S(2)}) copy-start(f32[512]{0:T(512)S(1)} %add_rsqrt_fusion.3) | copy-start | bytes 6148
  48.0 103.1 %copy-start.58 = (f32[1,1024]{1,0:T(1,128)}, f32[1,1024]{1,0:T(1,128)S(1)}, u32[]{:S(2)}) copy-start(f32[1,1024]{1,0:T(1,128)S(1)} %get-tuple-element.216) | copy-start | bytes 12292
  49.4 45.0 %collective-permute-start = (bf16[512,1024]{1,0:T(8,128)(2,1)}, bf16[512,1024]{1,0:T(8,128)(2,1)}, u32[]{:S(2)}, u32[]{:S(2)}) collective-permute-start(bf16[512,1024]{1,0:T(8,128)(2,1)} %fusion.69), channel_id=1, source_target_pairs={{0,1},{1,2},{2,3},{3,0},{4,5},{5,6},{6,7},{7,4},{8,9},{9,10},{10,1... | collective-permute-start | bytes 3145736 | tf_op jit(solution)/shard_map/ppermute | solution.py:18
  50.1 94.0 %collective-permute-start.2 = (bf16[512,1024]{1,0:T(8,128)(2,1)}, bf16[512,1024]{1,0:T(8,128)(2,1)}, u32[]{:S(2)}, u32[]{:S(2)}) collective-permute-start(bf16[512,1024]{1,0:T(8,128)(2,1)} %fusion.69), channel_id=1, source_target_pairs={{0,3},{1,0},{2,1},{3,2},{4,7},{5,4},{6,5},{7,6},{8,11},{9,8},{10,9... | collective-permute-start | bytes 3145736 | tf_op jit(solution)/shard_map/ppermute | solution.py:21
  94.4 43.7 %collective-permute-start.1 = (bf16[512,1024]{1,0:T(8,128)(2,1)}, bf16[512,1024]{1,0:T(8,128)(2,1)}, u32[]{:S(2)}, u32[]{:S(2)}) collective-permute-start(bf16[512,1024]{1,0:T(8,128)(2,1)} %collective-permute-done), channel_id=1, source_target_pairs={{0,1},{1,2},{2,3},{3,0},{4,5},{5,6},{6,7},{7,4},{8,9},{9,10},{10,1... | collective-permute-start | bytes 3145736 | tf_op jit(solution)/shard_map/ppermute | solution.py:18
  161.0 8.6 %copy-start.41 = (bf16[1024,256]{0,1:T(8,128)(2,1)}, bf16[1024,256]{0,1:T(8,128)(2,1)S(1)}, u32[]{:S(2)}) copy-start(bf16[1024,256]{0,1:T(8,128)(2,1)S(1)} %get-tuple-element.192) | copy-start | bytes 1572868
  162.0 12.0 %copy-start.32 = (bf16[512,256]{0,1:T(8,128)(2,1)}, bf16[512,256]{0,1:T(8,128)(2,1)S(1)}, u32[]{:S(2)}) copy-start(bf16[512,256]{0,1:T(8,128)(2,1)S(1)} %get-tuple-element.187) | copy-start | bytes 786436
  162.0 23.7 %copy-start.24 = (bf16[512,256]{0,1:T(8,128)(2,1)}, bf16[512,256]{0,1:T(8,128)(2,1)S(1)}, u32[]{:S(2)}) copy-start(bf16[512,256]{0,1:T(8,128)(2,1)S(1)} %get-tuple-element.186) | copy-start | bytes 786436
  163.1 11.0 %copy-start.16 = (bf16[1536,256]{0,1:T(8,128)(2,1)}, bf16[1536,256]{0,1:T(8,128)(2,1)S(1)}, u32[]{:S(2)}) copy-start(bf16[1536,256]{0,1:T(8,128)(2,1)S(1)} %get-tuple-element.193) | copy-start | bytes 2359300
  164.3 21.4 %copy-start.13 = (bf16[2048,256]{0,1:T(8,128)(2,1)}, bf16[2048,256]{0,1:T(8,128)(2,1)S(1)}, u32[]{:S(2)}) copy-start(bf16[2048,256]{0,1:T(8,128)(2,1)S(1)} %get-tuple-element.195) | copy-start | bytes 3145732
  193.5 8.2 %copy-start.18 = (bf16[2048,256]{0,1:T(8,128)(2,1)S(1)}, bf16[2048,256]{0,1:T(8,128)(2,1)}, u32[]{:S(2)}) copy-start(bf16[2048,256]{0,1:T(8,128)(2,1)} %get-tuple-element.196) | copy-start | bytes 3145732
  201.8 7.6 %copy-start.3 = (f32[4,512,512]{1,2,0:T(8,128)S(1)}, f32[4,512,512]{1,2,0:T(8,128)}, u32[]{:S(2)}) copy-start(f32[4,512,512]{1,2,0:T(8,128)} %copy-done.2) | copy-start | bytes 12582916
  201.8 7.6 %copy-start.45 = (bf16[512,256]{0,1:T(8,128)(2,1)S(1)}, bf16[512,256]{0,1:T(8,128)(2,1)}, u32[]{:S(2)}) copy-start(bf16[512,256]{0,1:T(8,128)(2,1)} %get-tuple-element.190) | copy-start | bytes 786436
  213.0 28.7 %all-to-all-start = ((bf16[4,512,256]{1,2,0:T(8,128)(2,1)}), bf16[4,512,256]{1,2,0:T(8,128)(2,1)S(1)}, u32[]{:S(2)}, u32[]{:S(2)}) async-start(bf16[4,512,256]{1,2,0:T(8,128)(2,1)} %copy.76), calls=%async_computation | async-start | bytes 2097152 | tf_op jit(solution)/shard_map/all_to_all | solution.py:208
  216.5 207.4 %reduce-scatter.13.cloned.1.call-start = ((), (), s32[]{:S(2)}) async-start(), calls=%async_computation.18 | async-start | bytes 2359296 | tf_op jit(solution)/shard_map/reduce_scatter | solution.py:244
  247.0 13.2 %copy-start.48 = (bf16[512,1024]{1,0:T(8,128)(2,1)}, bf16[512,1024]{1,0:T(8,128)(2,1)S(1)}, u32[]{:S(2)}) copy-start(bf16[512,1024]{1,0:T(8,128)(2,1)S(1)} %add_convert_fusion.1) | copy-start | bytes 3145732
  247.0 2.9 collective-permute-start.3
  276.2 2.7 collective-permute-start.6
  283.0 13.8 %copy-start.66 = (bf16[1024,2048]{0,1:T(8,128)(2,1)S(1)}, bf16[1024,2048]{0,1:T(8,128)(2,1)}, u32[]{:S(2)}) copy-start(bf16[1024,2048]{0,1:T(8,128)(2,1)} %all-gather.13.cloned.1.call-done) | copy-start | bytes 12582916
  283.0 2.7 collective-permute-start.7
  285.7 11.2 %copy-start.68 = (bf16[512,1024]{1,0:T(8,128)(2,1)}, bf16[512,1024]{1,0:T(8,128)(2,1)S(1)}, u32[]{:S(2)}) copy-start(bf16[512,1024]{1,0:T(8,128)(2,1)S(1)} %collective-permute-done.7) | copy-start | bytes 3145732
  303.3 2.7 collective-permute-start.8
  315.7 122.7 %reduce-scatter.21.cloned.1.call-start = ((), (), s32[]{:S(2)}) async-start(), calls=%async_computation.22 | async-start | bytes 5242880 | tf_op jit(solution)/shard_map/reduce_scatter | solution.py:179
  330.3 30.7 %all-to-all-start.1 = ((bf16[4,512,256]{2,1,0:T(8,128)(2,1)}), bf16[4,512,256]{2,1,0:T(8,128)(2,1)S(1)}, u32[]{:S(2)}, u32[]{:S(2)}) async-start(bf16[4,512,256]{2,1,0:T(8,128)(2,1)} %bitcast.200), calls=%async_computation.1 | async-start | bytes 2097152 | tf_op jit(solution)/shard_map/all_to_all | solution.py:241
  334.9 133.4 %reduce-scatter.17.cloned.1.call-start = ((), (), s32[]{:S(2)}) async-start(), calls=%async_computation.20 | async-start | bytes 5242880 | tf_op jit(solution)/shard_map/reduce_scatter | solution.py:179
  344.8 17.6 %copy-start.46 = (bf16[512,256]{0,1:T(8,128)(2,1)S(1)}, bf16[512,256]{0,1:T(8,128)(2,1)}, u32[]{:S(2)}) copy-start(bf16[512,256]{0,1:T(8,128)(2,1)} %get-tuple-element.190) | copy-start | bytes 786436
  344.8 148.0 %reduce-scatter.15.cloned.1.call-start = ((), (), s32[]{:S(2)}) async-start(), calls=%async_computation.19 | async-start | bytes 327680 | tf_op jit(solution)/shard_map/reduce_scatter | solution.py:246
  362.1 7.5 %copy-start.34 = (bf16[1,512,256]{1,2,0:T(8,128)(2,1)}, bf16[1,512,256]{1,2,0:T(8,128)(2,1)S(1)}, u32[]{:S(2)}) copy-start(bf16[1,512,256]{1,2,0:T(8,128)(2,1)S(1)} %copy.86) | copy-start | bytes 786436
  375.3 8.0 %slice-start.5 = ((s8[12582912]{0:T(1024)(128)(4,1)}), s8[4194304]{0:T(1024)(128)(4,1)S(1)}, s32[]{:S(2)}) async-start(s8[12582912]{0:T(1024)(128)(4,1)} %bitcast.203), calls=%async_computation.29 | async-start | bytes 8388608
  375.3 9.2 %slice-start.6 = ((s8[12582912]{0:T(1024)(128)(4,1)}), s8[4194304]{0:T(1024)(128)(4,1)S(1)}, s32[]{:S(2)}) async-start(s8[12582912]{0:T(1024)(128)(4,1)} %bitcast.203), calls=%async_computation.30 | async-start | bytes 8388608
  391.0 10.6 %copy-start.17 = (bf16[1536,256]{0,1:T(8,128)(2,1)S(1)}, bf16[1536,256]{0,1:T(8,128)(2,1)}, u32[]{:S(2)}) copy-start(bf16[1536,256]{0,1:T(8,128)(2,1)} %copy-done.16) | copy-start | bytes 2359300
  391.0 14.6 %slice-start = ((s8[16777216]{0:T(1024)(128)(4,1)}), s8[4194304]{0:T(1024)(128)(4,1)S(1)}, s32[]{:S(2)}) async-start(s8[16777216]{0:T(1024)(128)(4,1)} %bitcast.201), calls=%async_computation.24 | async-start | bytes 8388608
  391.0 14.6 %slice-start.1 = ((s8[16777216]{0:T(1024)(128)(4,1)}), s8[4194304]{0:T(1024)(128)(4,1)S(1)}, s32[]{:S(2)}) async-start(s8[16777216]{0:T(1024)(128)(4,1)} %bitcast.201), calls=%async_computation.25 | async-start | bytes 8388608
  391.0 14.6 %slice-start.2 = ((s8[16777216]{0:T(1024)(128)(4,1)}), s8[4194304]{0:T(1024)(128)(4,1)S(1)}, s32[]{:S(2)}) async-start(s8[16777216]{0:T(1024)(128)(4,1)} %bitcast.201), calls=%async_computation.26 | async-start | bytes 8388608
  413.6 12.4 %copy-start.21 = (bf16[1024,256]{0,1:T(8,128)(2,1)S(1)}, bf16[1024,256]{0,1:T(8,128)(2,1)}, u32[]{:S(2)}) copy-start(bf16[1024,256]{0,1:T(8,128)(2,1)} %copy-done.20) | copy-start | bytes 1572868
  423.9 8.1 %copy-start.35 = (bf16[1,512,256]{1,2,0:T(8,128)(2,1)S(1)}, bf16[1,512,256]{1,2,0:T(8,128)(2,1)}, u32[]{:S(2)}) copy-start(bf16[1,512,256]{1,2,0:T(8,128)(2,1)} %copy-done.34) | copy-start | bytes 786436
  425.8 92.4 %reduce-scatter.23.cloned.1.call-start = ((), (), s32[]{:S(2)}) async-start(), calls=%async_computation.23 | async-start | bytes 1310720 | tf_op jit(solution)/shard_map/reduce_scatter | solution.py:181
  440.9 105.3 %reduce-scatter.19.cloned.1.call-start = ((), (), s32[]{:S(2)}) async-start(), calls=%async_computation.21 | async-start | bytes 1310720 | tf_op jit(solution)/shard_map/reduce_scatter | solution.py:181
  457.3 13.6 %copy-start.52 = (bf16[512,4,64]{0,2,1:T(8,128)(2,1)S(1)}, bf16[512,4,64]{0,2,1:T(8,128)(2,1)}, u32[]{:S(2)}) copy-start(bf16[512,4,64]{0,2,1:T(8,128)(2,1)} %fusion.121) | copy-start | bytes 786436
  457.3 13.6 %copy-start.53 = (bf16[512,4,64]{0,2,1:T(8,128)(2,1)S(1)}, bf16[512,4,64]{0,2,1:T(8,128)(2,1)}, u32[]{:S(2)}) copy-start(bf16[512,4,64]{0,2,1:T(8,128)(2,1)} %fusion.114) | copy-start | bytes 786436
  457.3 13.6 %copy-start.54 = (bf16[512,4,64]{0,2,1:T(8,128)(2,1)S(1)}, bf16[512,4,64]{0,2,1:T(8,128)(2,1)}, u32[]{:S(2)}) copy-start(bf16[512,4,64]{0,2,1:T(8,128)(2,1)} %fusion.115) | copy-start | bytes 786436
  457.3 13.6 %copy-start.55 = (bf16[512,4,64]{0,2,1:T(8,128)(2,1)S(1)}, bf16[512,4,64]{0,2,1:T(8,128)(2,1)}, u32[]{:S(2)}) copy-start(bf16[512,4,64]{0,2,1:T(8,128)(2,1)} %fusion.120) | copy-start | bytes 786436
  470.5 115.8 %reduce-scatter.11.cloned.1.call-start = ((), (), s32[]{:S(2)}) async-start(), calls=%async_computation.17 | async-start | bytes 1769472 | tf_op jit(solution)/shard_map/reduce_scatter | solution.py:254
  471.0 8.2 %copy-start.44 = (bf16[2048,4,64]{0,2,1:T(8,128)(2,1)S(1)}, bf16[2048,4,64]{0,2,1:T(8,128)(2,1)}, u32[]{:S(2)}) copy-start(bf16[2048,4,64]{0,2,1:T(8,128)(2,1)} %fusion.63) | copy-start | bytes 3145732
  486.2 179.2 %reduce-scatter.9.cloned.1.call-start = ((), (), s32[]{:S(2)}) async-start(), calls=%async_computation.16 | async-start | bytes 5242880 | tf_op jit(solution)/shard_map/reduce_scatter | solution.py:252
  492.7 172.7 %copy-start.6 = (bf16[512,1024]{1,0:T(8,128)(2,1)S(1)}, bf16[512,1024]{1,0:T(8,128)(2,1)}, u32[]{:S(2)}) copy-start(bf16[512,1024]{1,0:T(8,128)(2,1)} %param.30) | copy-start | bytes 3145732
  492.7 172.7 %copy-start.59 = (f32[1,1024]{1,0:T(1,128)S(1)}, f32[1,1024]{1,0:T(1,128)}, u32[]{:S(2)}) copy-start(f32[1,1024]{1,0:T(1,128)} %copy-done.58) | copy-start | bytes 12292
  492.7 172.7 %copy-start.61 = (f32[512]{0:T(512)S(1)}, f32[512]{0:T(512)}, u32[]{:S(2)}) copy-start(f32[512]{0:T(512)} %copy-done.60) | copy-start | bytes 6148
  492.7 172.7 %copy-start.63 = (f32[512]{0:T(512)S(1)}, f32[512]{0:T(512)}, u32[]{:S(2)}) copy-start(f32[512]{0:T(512)} %copy-done.62) | copy-start | bytes 6148
  492.7 217.8 %copy-start.11 = (f32[512,1024]{1,0:T(8,128)S(1)}, f32[512,1024]{1,0:T(8,128)}, u32[]{:S(2)}) copy-start(f32[512,1024]{1,0:T(8,128)} %copy-done.10) | copy-start | bytes 6291460
  519.2 68.8 %collective-permute-start.10 = (bf16[128,512]{1,0:T(8,128)(2,1)S(1)}, bf16[128,512]{1,0:T(8,128)(2,1)}, u32[]{:S(2)}, u32[]{:S(2)}) collective-permute-start(bf16[128,512]{1,0:T(8,128)(2,1)S(1)} %get-tuple-element.204), channel_id=1, source_target_pairs={{0,4},{4,0},{1,5},{5,1},{2,6},{6,2},{3,7},{7,3},{8,12},{12,8},{9,1... | collective-permute-start | bytes 393224 | tf_op jit(solution)/shard_map/ppermute | solution.py:150
  547.8 44.1 %collective-permute-start.9 = (bf16[128,512]{1,0:T(8,128)(2,1)}, bf16[128,512]{1,0:T(8,128)(2,1)}, u32[]{:S(2)}, u32[]{:S(2)}) collective-permute-start(bf16[128,512]{1,0:T(8,128)(2,1)} %get-tuple-element.206), channel_id=1, source_target_pairs={{0,4},{4,0},{1,5},{5,1},{2,6},{6,2},{3,7},{7,3},{8,12},{12,8},{9,1... | collective-permute-start | bytes 393224 | tf_op jit(solution)/shard_map/ppermute | solution.py:150
  (43 other events, 149.8 us)
Sparse Core Ops, SparseCore 0:
  10.8 34.1 all-gather.10
  47.1 54.8 all-gather.14
  103.8 24.4 all-gather.6
  130.1 28.0 all-gather.8
  159.9 52.4 all-gather.12
  214.6 52.4 all-gather.16
  315.8 41.0 reduce-scatter.12
  359.9 52.6 reduce-scatter.20
  415.6 52.5 reduce-scatter.16
  470.3 19.9 reduce-scatter.14
  492.6 25.5 reduce-scatter.22
  520.4 25.7 reduce-scatter.18
  549.5 36.8 reduce-scatter.10
  588.5 76.7 reduce-scatter.8
